TPU v7x, 256 devices: a whole 4x4x8 slice. The times are simulated.
256 devices in a mesh: fsdp: 64 (over z, y_lo, x), tp: 4 (over y_hi, core).
Axes of the slice: x: 4, y: 4 (y_hi: 2, y_lo: 2; y = y_hi * 2 + y_lo), z: 8, core: 2. Of those that a mesh axis runs over, the one named last changes fastest.
Arguments:
- tokens: bfloat16 [1024, 4096], P('fsdp', 'tp'), may hold values from -6 to 6
- route_logits: bfloat16 [1024, 2], P('fsdp'), may hold values from -6 to 6
- route_ids: int32 [1024, 2], P('fsdp'), may hold values from 0 to 7, all different within a row; in each aligned block of 1024 rows (0 to 1023, 1024 to 2047, ...) at most 512 rows name the same one
- gate_codes: bfloat16 [8, 14336, 4096], P(None, 'fsdp', 'tp'), may hold values from -4 to 4
- gate_scales: float32 [8, 14336, 32], P(None, 'fsdp', 'tp'), may hold values from 0.008 to 0.03
- up_codes: bfloat16 [8, 14336, 4096], P(None, 'fsdp', 'tp'), may hold values from -4 to 4
- up_scales: float32 [8, 14336, 32], P(None, 'fsdp', 'tp'), may hold values from 0.008 to 0.03
- down_codes: bfloat16 [8, 14336, 4096], P(None, 'fsdp', 'tp'), may hold values from -4 to 4
- down_scales: float32 [8, 14336, 32], P(None, 'fsdp', 'tp'), may hold values from 0.004 to 0.016
Outputs:
- mixed: bfloat16 [1024, 4096], P('fsdp', 'tp')
Inputs may be any that keep to these rules, and one draw needn't show every extreme that they name: `route_ids`: each row names two different experts; over all 1024 rows no expert is named more than 512 times, a bound that some block reaches.
All inputs are finite; a program needn't handle non-finite values.
Results may differ from a plain program's by a relative error of at most 0.011.
Values may be sent and summed in bfloat16 or wider, within the bound.
A program may use at most 128 MiB of HBM per device.

v0:
```python
import jax
import jax.numpy as jnp
from jax import lax
from jax.sharding import PartitionSpec as P


def sent_together(arrays, axis, dim, along):
    ends, at = ([], 0)
    for a in arrays[:-1]:
        at += a.shape[along]
        ends.append(at)
    both = jnp.concatenate(arrays, axis=along)
    return tuple(jnp.split(lax.all_gather(both, axis, axis=dim, tiled=True), ends, axis=along))


def in_order(parts, dim):
    parts = jnp.moveaxis(parts, 0, dim)
    shape = parts.shape
    return parts.reshape(*shape[:dim], shape[dim] * shape[dim + 1], *shape[dim + 2 :])


def copy_for_each(shard, axis):
    peers = lax.axis_size(axis)
    return lax.all_to_all(
        jnp.broadcast_to(shard[None], (peers, *shard.shape)), axis, 0, 0, tiled=True
    )


def collect(shard, axis, dim):
    return in_order(copy_for_each(shard, axis), dim)


def cut_along(shard, dim, peers):
    shape = shard.shape
    parts = shard.reshape(*shape[:dim], peers, shape[dim] // peers, *shape[dim + 1 :])
    return jnp.moveaxis(parts, dim, 0)


def sum_at_owner(shard, axis, dim):
    peers = lax.axis_size(axis)
    parts = lax.all_to_all(cut_along(shard, dim, peers), axis, 0, 0, tiled=True)
    return jnp.sum(parts.astype(jnp.float32), axis=0)


def ordered_places(route_ids, experts):
    flat_ids = route_ids.reshape(-1)
    one_hot = (flat_ids[:, None] == jnp.arange(experts, dtype=jnp.int32)[None, :]).astype(jnp.int32)
    earlier = jnp.cumsum(one_hot, axis=0) - one_hot
    slot_rank = jnp.sum(earlier * one_hot, axis=1)
    group_sizes = jnp.sum(one_hot, axis=0)
    offsets = jnp.cumsum(group_sizes) - group_sizes
    start = jnp.sum(one_hot * offsets[None, :], axis=1)
    return (start + slot_rank, group_sizes)


def expand_cols(codes, scales):
    leading, row_count, col_count = codes.shape
    blocks = scales.shape[2]
    grouped = codes.astype(jnp.float32).reshape(leading, row_count, blocks, col_count // blocks)
    grouped = grouped * scales[:, :, :, None]
    return grouped.reshape(leading, row_count, col_count).astype(jnp.bfloat16)


def route_weights(route_logits):
    logits = route_logits.astype(jnp.float32)
    first_w = jax.nn.sigmoid(logits[:, 0] - logits[:, 1])
    second_w = jax.nn.sigmoid(logits[:, 1] - logits[:, 0])
    return (first_w[:, None], second_w[:, None])


def body(
    tokens,
    route_logits,
    route_ids,
    gate_codes,
    gate_scales,
    up_codes,
    up_scales,
    down_codes,
    down_scales,
):
    all_tokens, all_logits = sent_together((tokens, route_logits), "fsdp", 0, 1)
    all_ids = collect(route_ids, "fsdp", 0)
    experts = gate_codes.shape[0]
    token_count = all_tokens.shape[0]
    feature_count = all_tokens.shape[1]
    repeated = jnp.repeat(all_tokens, 2, axis=0)
    gate_w = expand_cols(gate_codes, gate_scales)
    up_w = expand_cols(up_codes, up_scales)
    down_w = expand_cols(down_codes, down_scales)
    places, group_sizes = ordered_places(all_ids, experts)
    row_total = 2 * token_count
    ordered = jnp.zeros((row_total, feature_count), jnp.bfloat16).at[places].set(repeated)
    gate_part = lax.ragged_dot(
        ordered, jnp.swapaxes(gate_w, 1, 2), group_sizes, preferred_element_type=jnp.float32
    )
    up_part = lax.ragged_dot(
        ordered, jnp.swapaxes(up_w, 1, 2), group_sizes, preferred_element_type=jnp.float32
    )
    gate_sum, up_sum = (
        sum_at_owner(gate_part.astype(jnp.bfloat16), "tp", 0),
        sum_at_owner(up_part.astype(jnp.bfloat16), "tp", 0),
    )
    hidden_share = (jax.nn.silu(gate_sum) * up_sum).astype(jnp.bfloat16)
    hidden = collect(hidden_share, "tp", 0)
    outputs = lax.ragged_dot(hidden, down_w, group_sizes, preferred_element_type=jnp.float32)
    routed = outputs[places].reshape(token_count, 2, feature_count)
    first_w, second_w = route_weights(all_logits)
    combined = routed[:, 0] * first_w + routed[:, 1] * second_w
    mixed = sum_at_owner(combined.astype(jnp.bfloat16), "fsdp", 0)
    return mixed.astype(jnp.bfloat16)


def solution(mesh):
    in_specs = (
        P("fsdp", "tp"),
        P("fsdp", None),
        P("fsdp", None),
        P(None, "fsdp", "tp"),
        P(None, "fsdp", "tp"),
        P(None, "fsdp", "tp"),
        P(None, "fsdp", "tp"),
        P(None, "fsdp", "tp"),
        P(None, "fsdp", "tp"),
    )
    out_specs = P("fsdp", "tp")
    return jax.shard_map(body, mesh=mesh, in_specs=in_specs, out_specs=out_specs, check_vma=False)
```

profile of v0, /device:TPU:1, one launch (start us, length us, event | category | flops | bytes accessed | tf_op | source)
XLA Modules:
  0.0 541.5 jit_solution(14765204949879776051)
XLA Ops:
  6.5 0.8 copy.41
  7.3 1.4 pad_maximum_fusion
  8.7 0.0 all-gather.2.cloned.1.call-update
  8.7 1.3 broadcast_in_dim.9
  10.0 13.5 %all-to-all-start = ((s32[64,16,2]{1,2,0:T(2,128)}), s32[64,16,2]{1,2,0:T(2,128)S(1)}, u32[]{:S(2)}, u32[]{:S(2)}) async-start(s32[64,16,2]{1,2,0:T(2,128)} %broadcast_in_dim.9), calls=%async_computation | async-start | bytes 131072 | tf_op jit(solution)/shard_map/all_to_all | solution.py:24
  23.5 6.3 %copy.42 = bf16[8,224,1024]{1,2,0:T(8,128)(2,1)} copy(bf16[8,224,1024]{2,1,0:T(8,128)(2,1)} %param.12) | data formatting | bytes 7340032 | tf_op args[3]
  29.9 0.0 copy-done
  29.9 4.9 fusion.1
  34.8 0.0 all-to-all-done
  34.8 0.4 copy.39
  35.3 0.3 eq.25
  35.5 0.3 eq.29
  35.8 0.6 convert_reduce_fusion.2
  36.5 1.5 ragged-dot-metadata
  38.0 0.8 reduce-window.18
  38.8 2.3 reduce-window.19
  41.1 0.3 slice_reduce_fusion
  41.4 0.2 reduce-window.20
  41.6 0.7 bitcast_subtract_fusion
  42.2 0.1 add_bitcast_fusion
  42.3 0.1 fusion.5
  42.5 223.7 %all-gather.2.cloned.1.call-done = bf16[1024,1026]{1,0:T(8,128)(2,1)} async-done(((bf16[16,1026]{1,0:T(8,128)(2,1)}), bf16[1024,1026]{1,0:T(8,128)(2,1)}) %all-gather.2.cloned.1.call-update) | async-done | bytes 2101264 | tf_op jit(solution)/shard_map/all_gather | solution.py:13
  266.1 1.6 slice-done
  267.7 3.5 broadcast_in_dim.10
  271.2 7.2 %reshape.139 = bf16[2048,1024]{1,0:T(8,128)(2,1)} reshape(bf16[1024,2,1024]{2,1,0:T(2,128)(2,1)} %broadcast_in_dim.10) | data formatting | bytes 8388608 | tf_op jit(solution)/shard_map/reshape | solution.py:87
  278.5 13.0 %scatter_custom_fusion = bf16[2048,1024]{1,0:T(8,128)(2,1)} fusion(s32[2048]{0:T(1024)S(1)} %bitcast.42, bf16[2048,1024]{1,0:T(8,128)(2,1)} %reshape.139, bf16[]{:T(256)} %constant.10.clone.1), kind=kCustom, calls=%fused_computation.8 | custom fusion | bytes 4194816 | tf_op jit(solution)/shard_map/scatter | solution.py:93
  291.5 13.5 %ragged-dot-none.2 = f32[2048,224]{1,0:T(8,128)} custom-call(s32[1]{0:T(128)} %get-tuple-element.5, s32[9]{0:T(128)} %get-tuple-element.6, s32[15]{0:T(128)} %get-tuple-element.7, s32[15]{0:T(128)} %get-tuple-element.8, s32[1]{0:T(128)} %get-tuple-element.5, bf16[2048,1024]{1,0:T(8,128)(2,1)} %scatter_custom_fusion, bf16[8,1024,224]{2,1,0:T(8,128)(2,1)} %bitcast.34), custom_call_target="tpu_custom_call" | custom-call | flops 939524096 | bytes 9699360 | tf_op jit(solution)/shard_map/ragged_dot_general/ragged-dot-none
  304.9 1.7 convert_element_type.57
  306.6 1.3 copy.43
  307.9 51.1 %all-to-all-start.1 = ((bf16[4,512,224]{1,2,0:T(8,128)(2,1)}), bf16[4,512,224]{1,2,0:T(8,128)(2,1)S(1)}, u32[]{:S(2)}, u32[]{:S(2)}) async-start(bf16[4,512,224]{1,2,0:T(8,128)(2,1)} %copy.43), calls=%async_computation.1 | async-start | bytes 1835008 | tf_op jit(solution)/shard_map/all_to_all | solution.py:41
  359.0 6.3 %copy.44 = bf16[8,224,1024]{1,2,0:T(8,128)(2,1)} copy(bf16[8,224,1024]{2,1,0:T(8,128)(2,1)} %param.14) | data formatting | bytes 7340032 | tf_op args[5]
  365.3 0.0 copy-done.1
  365.3 4.9 fusion
  370.3 13.5 %ragged-dot-none.1 = f32[2048,224]{1,0:T(8,128)} custom-call(s32[1]{0:T(128)} %get-tuple-element.5, s32[9]{0:T(128)} %get-tuple-element.6, s32[15]{0:T(128)} %get-tuple-element.7, s32[15]{0:T(128)} %get-tuple-element.8, s32[1]{0:T(128)} %get-tuple-element.5, bf16[2048,1024]{1,0:T(8,128)(2,1)} %scatter_custom_fusion, bf16[8,1024,224]{2,1,0:T(8,128)(2,1)} %bitcast.37), custom_call_target="tpu_custom_call" | custom-call | flops 939524096 | bytes 9699360 | tf_op jit(solution)/shard_map/ragged_dot_general/ragged-dot-none
  383.7 1.7 convert_element_type.61
  385.5 1.3 copy.45
  386.7 0.0 all-to-all-done.1
  386.7 4.8 all-to-all-start.2
  391.5 0.3 copy.47
  391.9 4.3 mul.92
  396.2 8.9 %mul.93 = f32[8,224,1024]{2,1,0:T(8,128)} reshape(f32[8,224,8,128]{3,2,1,0:T(8,128)} %mul.92) | data formatting | bytes 14680064 | tf_op jit(solution)/shard_map/mul | solution.py:60
  405.1 0.1 convert_reduce_fusion.1
  405.3 0.0 all-to-all-done.2
  405.3 0.1 convert_reduce_fusion
  405.4 0.1 multiply_convert_fusion.1
  405.5 1.0 broadcast_in_dim.11
  406.5 4.8 all-to-all-start.3
  411.3 7.4 %multiply_convert_fusion = bf16[8,224,1024]{2,1,0:T(8,128)(2,1)} fusion(f32[8,224,1024]{2,1,0:T(8,128)} %mul.93, bf16[8,224,1024]{2,1,0:T(8,128)(2,1)} %param.16), kind=kLoop, calls=%fused_computation.6 | loop fusion | flops 5505024 | bytes 14680064 | tf_op jit(solution)/shard_map/convert_element_type | solution.py:61
  418.8 0.0 slice-done.1
  418.8 0.1 copy.51
  418.9 0.1 divide_reduce_fusion.1
  419.0 0.1 mul.95
  419.0 0.1 mul.98
  419.1 5.8 %all-to-all-done.3 = bf16[4,512,224]{1,2,0:T(8,128)(2,1)S(1)} async-done(((bf16[4,512,224]{1,2,0:T(8,128)(2,1)}), bf16[4,512,224]{1,2,0:T(8,128)(2,1)S(1)}, u32[]{:S(2)}, u32[]{:S(2)}) %all-to-all-start.3) | async-done | bytes 917536 | tf_op jit(solution)/shard_map/all_to_all | solution.py:24
  424.9 1.3 copy.46
  426.2 14.1 %ragged-dot-none = f32[2048,1024]{1,0:T(8,128)} custom-call(s32[1]{0:T(128)} %get-tuple-element.5, s32[9]{0:T(128)} %get-tuple-element.6, s32[15]{0:T(128)} %get-tuple-element.7, s32[15]{0:T(128)} %get-tuple-element.8, s32[1]{0:T(128)} %get-tuple-element.5, bf16[2048,224]{1,0:T(8,128)(2,1)} %bitcast.40, bf16[8,224,1024]{2,1,0:T(8,128)(2,1)} %multiply_convert_fusion), custom_call_target="tpu_custom_call" | custom-call | flops 939524096 | bytes 12976160 | tf_op jit(solution)/shard_map/ragged_dot_general/ragged-dot-none
  440.3 15.2 %gather_fusion = f32[2048,1024]{1,0:T(8,128)} fusion(f32[2048,1024]{1,0:T(8,128)} %ragged-dot-none, s32[2048]{0:T(1024)S(1)} %broadcast_clamp_fusion), kind=kCustom, calls=%fused_computation | custom fusion | bytes 16785408 | tf_op jit(solution)/shard_map/gather | solution.py:107
  455.4 10.6 %reshape.126 = f32[1024,2,1024]{2,1,0:T(2,128)} reshape(f32[2048,1024]{1,0:T(8,128)} %gather_fusion) | data formatting | bytes 16777216 | tf_op jit(solution)/shard_map/reshape | solution.py:107
  466.0 9.8 %fusion.7 = (f32[1024,1,1024]{2,1,0:T(1,128)S(1)}, f32[1024,1,1024]{2,1,0:T(1,128)S(1)}) fusion(f32[1024,2,1024]{2,1,0:T(2,128)} %reshape.126), kind=kLoop, calls=%fused_computation.30 | loop fusion | bytes 16777216 | tf_op jit(solution)/shard_map/slice | solution.py:109
  475.8 1.0 copy.49
  476.8 1.0 copy.50
  477.8 0.6 add_convert_fusion
  478.4 55.3 %all_to_all.25 = bf16[64,16,1024]{2,1,0:T(8,128)(2,1)S(1)} all-to-all(bf16[64,16,1024]{2,1,0:T(8,128)(2,1)S(1)} %add_convert_fusion), channel_id=1, replica_groups=mesh['fsdp'=64,'tp'=4] {'fsdp'}, dimensions={0} | all-to-all | bytes 4194304 | tf_op jit(solution)/shard_map/all_to_all | solution.py:41
  533.7 1.0 reduce_sum.62
  (12 shorter events, 0.0 us)
Async XLA Ops:
  6.5 23.3 %copy-start = (f32[8,224,8]{1,2,0:T(8,128)S(1)}, f32[8,224,8]{1,2,0:T(8,128)}, u32[]{:S(2)}) copy-start(f32[8,224,8]{1,2,0:T(8,128)} %param.13) | copy-start | bytes 172036
  6.5 259.6 %all-gather.2.cloned.1.call-start = ((), (), s32[]{:S(2)}) async-start(), calls=%async_computation.5 | async-start | bytes 2396160 | tf_op jit(solution)/shard_map/all_gather | solution.py:13
  10.0 24.8 %all-to-all-start = ((s32[64,16,2]{1,2,0:T(2,128)}), s32[64,16,2]{1,2,0:T(2,128)S(1)}, u32[]{:S(2)}, u32[]{:S(2)}) async-start(s32[64,16,2]{1,2,0:T(2,128)} %broadcast_in_dim.9), calls=%async_computation | async-start | bytes 131072 | tf_op jit(solution)/shard_map/all_to_all | solution.py:24
  266.1 1.6 slice-start
  307.9 78.8 %all-to-all-start.1 = ((bf16[4,512,224]{1,2,0:T(8,128)(2,1)}), bf16[4,512,224]{1,2,0:T(8,128)(2,1)S(1)}, u32[]{:S(2)}, u32[]{:S(2)}) async-start(bf16[4,512,224]{1,2,0:T(8,128)(2,1)} %copy.43), calls=%async_computation.1 | async-start | bytes 1835008 | tf_op jit(solution)/shard_map/all_to_all | solution.py:41
  359.0 6.3 %copy-start.1 = (f32[8,224,8]{1,2,0:T(8,128)S(1)}, f32[8,224,8]{1,2,0:T(8,128)}, u32[]{:S(2)}) copy-start(f32[8,224,8]{1,2,0:T(8,128)} %param.15) | copy-start | bytes 172036
  383.7 7.8 %copy-start.2 = (f32[8,224,8]{1,2,0:T(8,128)S(1)}, f32[8,224,8]{1,2,0:T(8,128)}, u32[]{:S(2)}) copy-start(f32[8,224,8]{1,2,0:T(8,128)} %param.17) | copy-start | bytes 172036
  386.7 18.5 %all-to-all-start.2 = ((bf16[4,512,224]{1,2,0:T(8,128)(2,1)}), bf16[4,512,224]{1,2,0:T(8,128)(2,1)S(1)}, u32[]{:S(2)}, u32[]{:S(2)}) async-start(bf16[4,512,224]{1,2,0:T(8,128)(2,1)} %copy.45), calls=%async_computation.2 | async-start | bytes 1835008 | tf_op jit(solution)/shard_map/all_to_all | solution.py:41
  406.5 18.4 %all-to-all-start.3 = ((bf16[4,512,224]{1,2,0:T(8,128)(2,1)}), bf16[4,512,224]{1,2,0:T(8,128)(2,1)S(1)}, u32[]{:S(2)}, u32[]{:S(2)}) async-start(bf16[4,512,224]{1,2,0:T(8,128)(2,1)} %broadcast_in_dim.11), calls=%async_computation.3 | async-start | bytes 1835008 | tf_op jit(solution)/shard_map/all_to_all | solution.py:24
  411.3 7.4 %slice-start.1 = ((bf16[1024,1026]{1,0:T(8,128)(2,1)}), bf16[1024,2]{1,0:T(8,128)(2,1)S(1)}, s32[]{:S(2)}) async-start(bf16[1024,1026]{1,0:T(8,128)(2,1)} %all-gather.2.cloned.1.call-done), calls=%async_computation.7 | async-start | bytes 524288 | tf_op jit(solution)/shard_map/split | solution.py:13
Sparse Core Ops, SparseCore 0:
  9.1 256.9 all-gather.1
where the time goes:
time: 547 us; the launch traced here: 541 us
  waiting for transfers between devices  229 us (42%)
  local copies, waits for them, and re-layouts  97.6 us (18%)
  starting transfers between devices  74.1 us (14%)
  blocking collectives  55.3 us (10%)
  Pallas kernels  42.5 us (8%)
  other arithmetic  28.9 us (5%)
  between operations  13.5 us (2%)
    all_gather x1, waiting for transfers between devices, sent_together(): lax.all_gather(both, axis, axis=dim, tiled=True)  224 us
    all_to_all x2, starting transfers between devices, sum_at_owner(): parts = lax.all_to_all(cut_along(shard, dim, peers), axis, 0, 0, tiled=True)  55.9 us
    all_to_all x1, blocking collectives, sum_at_owner(): parts = lax.all_to_all(cut_along(shard, dim, peers), axis, 0, 0, tiled=True)  55.3 us
    another operation x3, Pallas kernels  41 us
    all_to_all x2, starting transfers between devices, copy_for_each(): lax.all_to_all(jnp.broadcast_to(shard[None], (peers, *shard.shape)), axis...  18.3 us
    convert_element_type x3, other arithmetic, expand_cols(): return grouped.reshape(leading, row_count, col_count).astype(jnp.bfloat16)  17.3 us
    unnamed x13, local copies, waits for them, and re-layouts  15.9 us
    gather x1, local copies, waits for them, and re-layouts, body(): routed = outputs[places].reshape(token_count, 2, feature_count)  15.2 us
  transfers between devices with their start and end apart: 5, of which 2 were waited for; matrix products, arithmetic and copies ran while one was open for 10% of the time, Pallas kernels for 3%

commit v1 on v0

v1 whole, which is shorter than its diff:
```python
import jax
import jax.numpy as jnp
from jax import lax
from jax.experimental import pallas as pl
from jax.experimental.pallas import tpu as pltpu
from jax.sharding import PartitionSpec as P

F32, BF16 = jnp.float32, jnp.bfloat16
MESH = pl.DeviceIdType.MESH
E, FH, DK = 8, 224, 1024
XW = DK + 128
HW = DK // 2
OFFSETS = (0, 1, -1, 2, -2, 3, -3, 4)


def pos_of(r):
    return OFFSETS.index(r)


def kernel(
    tok_ref, log_ref, ids_ref, gc_ref, gs_ref, uc_ref, us_ref, dc_ref, ds_ref,
    out_ref,
    wgu, dw, sg, su, sd, xbuf, xt, acc, rt, pb, rb, yb, yr, hb, am, part, r1, s2, r2, zs, rz,
    w_sem, s_sem, p_send, p_recv, g_send, g_recv, t_send, t_recv, x_send, x_recv, z_send, z_recv,
):
    f, t = lax.axis_index("fsdp"), lax.axis_index("tp")
    z, blk = f // 8, f % 8
    y, x = blk // 4, blk % 4
    yh, core = t // 2, t % 2
    xa = x + 1 - 2 * (x % 2)
    xb = 3 - x
    xd = 3 - xa

    def fid(zz, yy, xx):
        return (zz * 2 + yy) * 4 + xx

    def dev(ff, tt):
        return {"fsdp": ff, "tp": tt}

    def zoff(r):
        return (z + r + 8) % 8

    sibling = dev(f, yh * 2 + 1 - core)
    partner = dev(f, (1 - yh) * 2 + core)
    sends = []

    def copy(src, dst, ssem, rsem, to):
        return pltpu.make_async_remote_copy(
            src_ref=src, dst_ref=dst, send_sem=ssem, recv_sem=rsem, device_id=to, device_id_type=MESH
        )

    def send(src, dst, ssem, rsem, to):
        c = copy(src, dst, ssem, rsem, to)
        c.start()
        sends.append(c)

    def arrived(dst, ssem, rsem):
        copy(dst, dst, ssem, rsem, sibling).wait_recv()

    def w_copy(kind, e):
        src = (gc_ref, uc_ref, dc_ref)[kind]
        dst = (wgu.at[e, pl.ds(0, FH)], wgu.at[e, pl.ds(FH, FH)], dw.at[e, pl.ds(0, FH)])[kind]
        return pltpu.make_async_copy(src.at[e], dst, w_sem.at[kind, e])

    def s_copy(kind):
        src, dst = ((gs_ref, sg), (us_ref, su), (ds_ref, sd))[kind]
        return pltpu.make_async_copy(src, dst, s_sem.at[kind])

    s_copy(0).start()
    s_copy(1).start()
    for kind in (0, 1, 2):
        if kind == 2:
            s_copy(2).start()

        @pl.loop(0, E)
        def _(e):
            w_copy(kind, e).start()

    lane = lax.broadcasted_iota(jnp.int32, (16, 128), 1)
    ids = ids_ref[...].astype(F32)
    logits = log_ref[...].astype(F32)
    extra = jnp.where(
        lane == 0,
        ids[:, 0:1],
        jnp.where(lane == 1, ids[:, 1:2], jnp.where(lane == 2, logits[:, 0:1], jnp.where(lane == 3, logits[:, 1:2], 0.0))),
    )
    xbuf[0, blk, :, 0:DK] = tok_ref[...]
    xbuf[0, blk, :, DK:XW] = extra.astype(BF16)

    barrier = pltpu.get_barrier_semaphore()
    friends = [dev(z * 8 + (blk + d) % 8, t) for d in range(1, 8)]
    friends += [dev(fid(zoff(r), yy, x), t) for r in OFFSETS[1:] for yy in (y, 1 - y)]
    friends += [sibling, partner]
    for to in friends:
        pl.semaphore_signal(barrier, inc=1, device_id=to, device_id_type=MESH)
    pl.semaphore_wait(barrier, len(friends))

    for d in range(1, 8):
        send(xbuf.at[0, blk], xbuf.at[0, blk], p_send.at[d], p_recv.at[d], dev(z * 8 + (blk + d) % 8, t))

    def plane_arrived():
        for d in range(1, 8):
            arrived(xbuf.at[0, (blk + 8 - d) % 8], p_send.at[d], p_recv.at[d])

    def ring_piece(way, s, p):
        return (p_of(way, s), pl.ds(4 * p, 4))

    def p_of(way, s):
        if s == 0:
            return 0
        return pos_of(4) if s == 4 else pos_of(-s if way == 0 else s)

    def ring(s, p):
        for way in (0, 1):
            if s > 1:
                at, rows = ring_piece(way, s - 1, p)
                arrived(xbuf.at[at, rows], g_send.at[way, s - 1, p], g_recv.at[way, s - 1, p])
            if s < 4 or p == way:
                a, rows = ring_piece(way, s - 1, p)
                b, _ = ring_piece(way, s, p)
                to = dev(fid(zoff(1 if way == 0 else -1), y, x), t)
                send(xbuf.at[a, rows], xbuf.at[b, rows], g_send.at[way, s, p], g_recv.at[way, s, p], to)

    def ring_end():
        for way in (0, 1):
            at, rows = ring_piece(way, 4, way)
            arrived(xbuf.at[at, rows], g_send.at[way, 4, way], g_recv.at[way, 4, way])

    def scale_gate_up(lo, hi):
        @pl.loop(lo, hi)
        def _(e):
            w_copy(0, e).wait()
            w_copy(1, e).wait()
            for at, sc in ((0, sg), (FH, su)):
                for b in range(8):
                    cols = slice(b * 128, (b + 1) * 128)
                    w = wgu[e, at : at + FH, cols].astype(F32) * sc[e, :, b : b + 1]
                    wgu[e, at : at + FH, cols] = w.astype(BF16)

    def scale_down(lo, hi):
        @pl.loop(lo, hi)
        def _(e):
            w_copy(2, e).wait()
            dw[e, FH:256, :] = jnp.zeros((256 - FH, DK), BF16)
            for b in range(8):
                cols = slice(b * 128, (b + 1) * 128)
                w = dw[e, 0:FH, cols].astype(F32) * sd[e, :, b : b + 1]
                dw[e, 0:FH, cols] = w.astype(BF16)

    def gate_up(c):
        rows = xbuf[2 * c : 2 * c + 2].reshape(256, XW)
        xt[...] = rows[:, 0:DK].T
        route = rows[:, DK:XW].astype(F32).T
        for hh in (0, 1):
            rt[c, hh] = route[0:8, hh * 128 : (hh + 1) * 128]
        picks = [[route[k : k + 1, hh * 128 : (hh + 1) * 128] for hh in (0, 1)] for k in (0, 1)]

        def one(e):
            o = jnp.dot(wgu[e], xt[...], preferred_element_type=F32)
            for k in (0, 1):
                for hh in (0, 1):
                    mine = o[:, hh * 128 : (hh + 1) * 128]
                    hit = picks[k][hh] == jnp.asarray(e, jnp.int32).astype(F32)
                    acc[c, k, hh] = jnp.where(hit, mine, 0.0 if isinstance(e, int) else acc[c, k, hh])

        one(0)
        pl.loop(1, E)(one)
        pb[c] = acc[c, 1 - core].astype(BF16)
        send(pb.at[c], rb.at[c], t_send.at[0, c], t_recv.at[0, c], sibling)

    def pair_sum(c, hh):
        return acc[c, core, hh] + rb[c, hh].astype(F32)

    def core_sum(c):
        arrived(rb.at[c], t_send.at[0, c], t_recv.at[0, c])
        yb[c] = pair_sum(c, 1 - yh).astype(BF16)
        send(yb.at[c], yr.at[c], t_send.at[1, c], t_recv.at[1, c], partner)

    def activate(c):
        arrived(yr.at[c], t_send.at[1, c], t_recv.at[1, c])
        total = pair_sum(c, yh) + yr[c].astype(F32)
        gate, up = total[0:FH], total[FH : 2 * FH]
        route = rt[c, yh]
        diff = route[3:4] - route[2:3]
        w = 1.0 / (1.0 + jnp.exp(jnp.where(core == 0, diff, -diff)))
        hb[c, core, yh] = (gate / (1.0 + jnp.exp(-gate)) * up * w).astype(BF16)
        mine = hb.at[c, core, yh]
        send(mine, mine, t_send.at[2, c], t_recv.at[2, c], partner)
        send(mine, mine, t_send.at[3, c], t_recv.at[3, c], sibling)

    def pass_on(c):
        theirs = hb.at[c, core, 1 - yh]
        arrived(theirs, t_send.at[2, c], t_recv.at[2, c])
        send(theirs, theirs, t_send.at[4, c], t_recv.at[4, c], sibling)

    def down(c):
        arrived(hb.at[c, 1 - core, yh], t_send.at[3, c], t_recv.at[3, c])
        arrived(hb.at[c, 1 - core, 1 - yh], t_send.at[4, c], t_recv.at[4, c])
        pad = jnp.zeros((256 - FH, 128), F32)
        for hh in (0, 1):
            here = slice(hh * 128, (hh + 1) * 128)
            route = xbuf[2 * c + hh, :, :, DK:XW].reshape(128, 128).astype(F32)
            units = [jnp.concatenate([hb[c, k, hh].astype(F32), pad], axis=0).T for k in (0, 1)]
            for e in range(E):
                both = jnp.where(route[:, 0:1] == float(e), units[0], 0.0)
                both = jnp.where(route[:, 1:2] == float(e), units[1], both)
                am[here, e * 256 : (e + 1) * 256] = both.astype(BF16)
        for j in range(4):
            w = dw[:, :, j * 256 : (j + 1) * 256].reshape(E * 256, 256)
            o = jnp.dot(am[...], w, preferred_element_type=F32)
            half, at = j // 2, (j % 2) * 256
            part[half, 2 * c : 2 * c + 2, :, :, :, at : at + 256] = o.astype(BF16).reshape(2, 2, 4, 16, 256)
        two = pl.ds(2 * c, 2)
        for half, first in ((0, xa), (1, xb)):
            for j, at in ((0, first), (1, xd)):
                send(
                    part.at[half, two, :, at], r1.at[half, two, :, j],
                    x_send.at[c, half, j], x_recv.at[c, half, j], dev(fid(z, y, first), t),
                )

    def x_first(c):
        two = pl.ds(2 * c, 2)
        for half, second in ((0, xb), (1, xa)):
            for j in (0, 1):
                arrived(r1.at[half, two, :, j], x_send.at[c, half, j], x_recv.at[c, half, j])
            s2[half, two] = (part[half, two, :, second].astype(F32) + r1[half, two, :, 1].astype(F32)).astype(BF16)
            send(
                s2.at[half, two], r2.at[half, two],
                x_send.at[c, half, 2], x_recv.at[c, half, 2], dev(fid(z, y, second), t),
            )

    def x_second(c):
        two = pl.ds(2 * c, 2)
        for half in (0, 1):
            arrived(r2.at[half, two], x_send.at[c, half, 2], x_recv.at[c, half, 2])
            total = part[half, two, :, x].astype(F32) + r1[half, two, :, 0].astype(F32) + r2[half, two].astype(F32)
            zs[two, :, half] = total.astype(BF16)
        for at in (2 * c, 2 * c + 1):
            for dy in (0, 1):
                if at or dy:
                    yy = (y + dy) % 2
                    to = dev(fid(zoff(OFFSETS[at]), yy, x), t)
                    send(zs.at[at, yy], rz.at[at, dy], z_send.at[at, dy], z_recv.at[at, dy], to)

    def finish():
        total = zs[0, y].astype(F32)
        for at in range(8):
            for dy in (0, 1):
                if at or dy:
                    arrived(rz.at[at, dy], z_send.at[at, dy], z_recv.at[at, dy])
                    total = total + rz[at, dy].astype(F32)
        for half in (0, 1):
            out_ref[:, half * HW : (half + 1) * HW] = total[half].astype(BF16)

    s_copy(0).wait()
    s_copy(1).wait()
    scale_gate_up(0, 2)
    plane_arrived()
    ring(1, 0), ring(1, 1)
    scale_gate_up(2, 8)
    ring(2, 0), ring(2, 1)
    gate_up(0)
    ring(3, 0)
    s_copy(2).wait()
    scale_down(0, 4)
    core_sum(0)
    ring(3, 1)
    gate_up(1)
    ring(4, 0)
    scale_down(4, 8)
    activate(0), core_sum(1)
    ring(4, 1)
    pass_on(0)
    gate_up(2)
    down(0)
    activate(1), core_sum(2)
    ring_end()
    gate_up(3)
    pass_on(1)
    x_first(0)
    down(1)
    core_sum(3), activate(2)
    x_second(0)
    x_first(1)
    pass_on(2)
    down(2)
    activate(3)
    x_second(1)
    pass_on(3)
    x_first(2)
    down(3)
    x_second(2)
    x_first(3)
    x_second(3)
    finish()
    for c in sends:
        c.wait_send()


def body(tokens, logits, ids, gate_codes, gate_scales, up_codes, up_scales, down_codes, down_scales):
    vmem = pl.BlockSpec(memory_space=pltpu.VMEM)
    hbm = pl.BlockSpec(memory_space=pl.ANY)
    sems = pltpu.SemaphoreType.DMA
    return pl.pallas_call(
        kernel,
        out_shape=jax.ShapeDtypeStruct((16, DK), BF16),
        in_specs=[vmem] * 3 + [hbm] * 6,
        out_specs=vmem,
        scratch_shapes=[
            pltpu.VMEM((E, 2 * FH, DK), BF16),
            pltpu.VMEM((E, 256, DK), BF16),
            pltpu.VMEM((E, FH, 8), F32),
            pltpu.VMEM((E, FH, 8), F32),
            pltpu.VMEM((E, FH, 8), F32),
            pltpu.VMEM((8, 8, 16, XW), BF16),
            pltpu.VMEM((DK, 256), BF16),
            pltpu.VMEM((4, 2, 2, 2 * FH, 128), F32),
            pltpu.VMEM((4, 2, 8, 128), F32),
            pltpu.VMEM((4, 2, 2 * FH, 128), BF16),
            pltpu.VMEM((4, 2, 2 * FH, 128), BF16),
            pltpu.VMEM((4, 2 * FH, 128), BF16),
            pltpu.VMEM((4, 2 * FH, 128), BF16),
            pltpu.VMEM((4, 2, 2, FH, 128), BF16),
            pltpu.VMEM((256, E * 256), BF16),
            pltpu.VMEM((2, 8, 2, 4, 16, HW), BF16),
            pltpu.VMEM((2, 8, 2, 2, 16, HW), BF16),
            pltpu.VMEM((2, 8, 2, 16, HW), BF16),
            pltpu.VMEM((2, 8, 2, 16, HW), BF16),
            pltpu.VMEM((8, 2, 2, 16, HW), BF16),
            pltpu.VMEM((8, 2, 2, 16, HW), BF16),
            sems((3, E)),
            sems((3,)),
            sems((8,)),
            sems((8,)),
            sems((2, 5, 2)),
            sems((2, 5, 2)),
            sems((5, 4)),
            sems((5, 4)),
            sems((4, 2, 3)),
            sems((4, 2, 3)),
            sems((8, 2)),
            sems((8, 2)),
        ],
        compiler_params=pltpu.CompilerParams(
            collective_id=0, has_side_effects=True, vmem_limit_bytes=60 * 1024 * 1024
        ),
        name="expert_step",
    )(tokens, logits, ids, gate_codes, gate_scales, up_codes, up_scales, down_codes, down_scales)


def solution(mesh):
    wide = P(None, "fsdp", "tp")
    in_specs = (P("fsdp", "tp"), P("fsdp", None), P("fsdp", None)) + (wide,) * 6
    return jax.shard_map(body, mesh=mesh, in_specs=in_specs, out_specs=P("fsdp", "tp"), check_vma=False)
```

time: 547 us -> 100 us (0.18)
  the two profiles are of different devices: /device:TPU:1 before, /device:TPU:104 now
where the time goes in v1:
time: 100 us; the launch traced here: 99.8 us
  Pallas kernels  89.4 us (89%)
  local copies, waits for them, and re-layouts  10.3 us (10%)
    pallas_call x1, Pallas kernels, body(): pl.pallas_call(kernel, out_shape=jax.ShapeDtypeStruct((16, DK), BF16), in...  89.4 us
    unnamed x6, local copies, waits for them, and re-layouts  10.3 us

profile of v1, /device:TPU:104, one launch (start us, length us, event | category | flops | bytes accessed | tf_op | source)
XLA Modules:
  0.0 99.8 jit_solution(7040280169514793796)
XLA Ops:
  0.0 1.3 %copy.10.log_ref = bf16[16,2]{1,0:T(8,128)(2,1)} copy(bf16[16,2]{0,1:T(2,128)(2,1)} %param.10) | data formatting | bytes 128 | tf_op args[1]
  1.3 1.4 %copy.11.ids_ref = s32[16,2]{1,0:T(8,128)} copy(s32[16,2]{0,1:T(2,128)} %param.11) | data formatting | bytes 256 | tf_op args[2]
  2.7 2.1 %copy.12.gs_ref = f32[8,224,8]{2,1,0:T(8,128)} copy(f32[8,224,8]{1,2,0:T(8,128)} %param.13) | data formatting | bytes 114688 | tf_op args[4]
  4.8 2.1 %copy.13.us_ref = f32[8,224,8]{2,1,0:T(8,128)} copy(f32[8,224,8]{1,2,0:T(8,128)} %param.15) | data formatting | bytes 114688 | tf_op args[6]
  6.9 2.1 %copy.14.ds_ref = f32[8,224,8]{2,1,0:T(8,128)} copy(f32[8,224,8]{1,2,0:T(8,128)} %param.17) | data formatting | bytes 114688 | tf_op args[8]
  9.0 89.4 %expert_step.1 = bf16[16,1024]{1,0:T(8,128)(2,1)} custom-call(bf16[16,1024]{1,0:T(8,128)(2,1)} %tok_ref.1, bf16[16,2]{1,0:T(8,128)(2,1)} %copy.10.log_ref, s32[16,2]{1,0:T(8,128)} %copy.11.ids_ref, bf16[8,224,1024]{2,1,0:T(8,128)(2,1)} %gc_ref.1, f32[8,224,8]{2,1,0:T(8,128)} %copy.12.gs_ref, bf16[8,224,1024]{2,1,0:T(8,128)(2,1)} %uc_ref.1, ...), custom_call_target="tpu_custom_call" | custom-call | tf_op jit(solution)/shard_map/expert_step/pallas_call | solution.py:304
  98.4 1.4 %copy.16 = bf16[16,1024]{1,0:T(8,128)(2,1)} copy(bf16[16,1024]{1,0:T(8,128)(2,1)} %expert_step.1) | data formatting | bytes 65536

commit v2 on v1

v2 whole, which is shorter than its diff:
```python
import jax
import jax.numpy as jnp
from jax import lax
from jax.experimental import pallas as pl
from jax.experimental.pallas import tpu as pltpu
from jax.sharding import PartitionSpec as P

F32, BF16 = jnp.float32, jnp.bfloat16
MESH = pl.DeviceIdType.MESH
E, FH, DK = 8, 224, 1024
GROUP = 4
HW = DK // 2
OFFSETS = (1, -1, 3, -3, 4, 2, -2, 0)


def pos_of(r):
    return OFFSETS.index(r)


def kernel(
    tok_ref, log_ref, ids_ref, gc_ref, gs_ref, uc_ref, us_ref, dc_ref, ds_ref,
    out_ref,
    wgu, dw, sc, tgu, td, flip, xbuf, rbuf, xt, acc, rt, pb, rb, yb, yr, hb, am, part, r1, s2, r2, zs, rz,
    w_sem, out_sem, g_recv, h_recv, t_recv, x_recv, z_recv,
):
    f, t = lax.axis_index("fsdp"), lax.axis_index("tp")
    z, blk = f // 8, f % 8
    y, x = blk // 4, blk % 4
    yh, core = t // 2, t % 2
    xa = x + 1 - 2 * (x % 2)
    xb = 3 - x
    xd = 3 - xa
    left, right, far = (x + 3) % 4, (x + 1) % 4, (x + 2) % 4
    own = pos_of(0)

    def fid(zz, yy, xx):
        return (zz * 2 + yy) * 4 + xx

    def dev(ff, tt):
        return {"fsdp": ff, "tp": tt}

    def zoff(r):
        return (z + r + 8) % 8

    sibling = dev(f, yh * 2 + 1 - core)
    partner = dev(f, (1 - yh) * 2 + core)

    def copy(src, dst, ssem, rsem, to):
        return pltpu.make_async_remote_copy(
            src_ref=src, dst_ref=dst, send_sem=ssem, recv_sem=rsem, device_id=to, device_id_type=MESH
        )

    G, H, PB, YB, HB, X1, X2, Z = range(8)

    def send(src, dst, kind, rsem, to):
        copy(src, dst, out_sem.at[kind], rsem, to).start()

    def arrived(dst, rsem):
        copy(dst, dst, out_sem.at[G], rsem, sibling).wait_recv()

    def all_sent(src, kind):
        copy(src, src, out_sem.at[kind], out_sem.at[kind], sibling).wait_send()

    barrier = pltpu.get_barrier_semaphore()
    friends = [dev(fid(zoff(r), (y + dy) % 2, x), t) for r in OFFSETS for dy in (0, 1) if r or dy]
    friends += [dev(fid(z, y, left), t), dev(fid(z, y, right), t), sibling, partner]
    for to in friends:
        pl.semaphore_signal(barrier, inc=1, device_id=to, device_id_type=MESH)

    def w_copy(kind):
        src = (gc_ref, uc_ref, dc_ref)[kind]
        dst = (wgu.at[:, pl.ds(0, FH)], wgu.at[:, pl.ds(FH, FH)], dw.at[:, pl.ds(0, FH)])[kind]
        return pltpu.make_async_copy(src, dst, w_sem.at[kind])

    def s_copy(kind):
        return pltpu.make_async_copy((gs_ref, us_ref, ds_ref)[kind], sc.at[kind], w_sem.at[3 + kind])

    for kind in range(3):
        s_copy(kind).start()
    for kind in range(3):
        w_copy(kind).start()

    flip[...] = jnp.zeros((8, 128), F32)
    flip[0:2, 0:16] = ids_ref[...].astype(F32)
    flip[2:4, 0:16] = log_ref[...].astype(F32)
    xbuf[own, y, x] = tok_ref[...]
    rbuf[own, y, x] = jnp.sum(pltpu.roll(flip[...], 0, 1, stride=16, stride_axis=0), axis=0, keepdims=True)

    def enter():
        pl.semaphore_wait(barrier, len(friends))

    def both(src, dst, kind, at, to, routes=True):
        send(xbuf.at[src], xbuf.at[dst], G, g_recv.at[kind, at], to)
        if routes:
            send(rbuf.at[src[:3]], rbuf.at[dst[:3]], H, h_recv.at[kind, at], to)

    every = slice(None)
    low, high = slice(0, HW), slice(HW, DK)

    def spread():
        for at, r in enumerate(OFFSETS):
            for dy in (0, 1):
                if r or dy:
                    both((own, y, x), (at, y, x), 0, at, dev(fid(zoff(-r), (y + dy) % 2, x), t))

    def along_x(at):
        rows = every if OFFSETS[at] else 1 - y
        arrived(xbuf.at[at, rows, x], g_recv.at[0, at])
        arrived(rbuf.at[at, rows, x], h_recv.at[0, at])
        for to in (right, left):
            both((at, every, x), (at, every, x), 1, at, dev(fid(z, y, to), t))

    def along_x_again(at):
        arrived(xbuf.at[at, 0], g_recv.at[1, at])
        arrived(rbuf.at[at, 0], h_recv.at[1, at])
        here = (at, every, left, every, low)
        both(here, here, 2, at, dev(fid(z, y, right), t))
        here = (at, every, right, every, high)
        both(here, here, 2, at, dev(fid(z, y, left), t), False)

    def plane_complete(at):
        arrived(xbuf.at[at, every, far], g_recv.at[2, at])
        arrived(rbuf.at[at, every, far], h_recv.at[2, at])

    lanes = lax.broadcasted_iota(jnp.int32, (8, 128), 1) // 16
    on_row = lanes == lax.broadcasted_iota(jnp.int32, (8, 128), 0)

    def unpack_routes(at):
        rows = jnp.concatenate([rbuf[at, i // 4, i % 4] for i in range(8)], axis=0)
        rows = pltpu.roll(rows, 0, 1, stride=16, stride_axis=0)
        for v in range(4):
            turned = pltpu.roll(rows, 128 - 16 * v, 1) if v else rows
            rt[at // 2, at % 2, v : v + 1, :] = jnp.sum(jnp.where(on_row, turned, 0.0), axis=0, keepdims=True)

    def turn_scales():
        for kind in range(3):
            s_copy(kind).wait()
        for kinds, dst in ((slice(0, 2), tgu), (slice(2, 3), td)):
            rows = sc[kinds].reshape(-1, FH)
            if rows.shape[0] < 128:
                rows = jnp.concatenate([rows, jnp.zeros((128 - rows.shape[0], FH), F32)], axis=0)
            dst[0:128] = rows[:, 0:128].T
            dst[128:FH] = jnp.concatenate([rows[:, 128:FH], jnp.zeros((128, 256 - FH), F32)], axis=1).T[0 : FH - 128]
        for kind in range(3):
            w_copy(kind).wait()

    def scale_gate_up(lo, hi):
        @pl.loop(lo, hi)
        def _(e):
            scales = pltpu.roll(tgu[...], (128 - 8 * e) % 128, 1)
            for at, lane in ((0, 0), (FH, 64)):
                for b in range(8):
                    cols = slice(b * 128, (b + 1) * 128)
                    w = wgu[e, at : at + FH, cols].astype(F32) * scales[:, lane + b : lane + b + 1]
                    wgu[e, at : at + FH, cols] = w.astype(BF16)

    def scale_down(lo, hi):
        @pl.loop(lo, hi)
        def _(e):
            dw[e, FH:256, :] = jnp.zeros((256 - FH, DK), BF16)
            scales = pltpu.roll(td[...], (128 - 8 * e) % 128, 1)
            for b in range(8):
                cols = slice(b * 128, (b + 1) * 128)
                w = dw[e, 0:FH, cols].astype(F32) * scales[:, b : b + 1]
                dw[e, 0:FH, cols] = w.astype(BF16)

    def gate_up(c):
        for hh in (0, 1):
            plane_complete(2 * c + hh)
            unpack_routes(2 * c + hh)
        xt[...] = xbuf[2 * c : 2 * c + 2].reshape(256, DK).T
        picks = [[rt[c, hh, k : k + 1, :] for hh in (0, 1)] for k in (0, 1)]

        @pl.loop(0, E // GROUP)
        def _(g):
            w = wgu[pl.ds(g * GROUP, GROUP)].reshape(GROUP * 2 * FH, DK)
            o = jnp.dot(w, xt[...], preferred_element_type=F32)
            for i in range(GROUP):
                e = jnp.asarray(g * GROUP + i, jnp.int32).astype(F32)
                for k in (0, 1):
                    for hh in (0, 1):
                        mine = o[i * 2 * FH : (i + 1) * 2 * FH, hh * 128 : (hh + 1) * 128]
                        acc[c, k, hh] = jnp.where(picks[k][hh] == e, mine, acc[c, k, hh])

        pb[c] = acc[c, 1 - core].astype(BF16)
        send(pb.at[c], rb.at[c], PB, t_recv.at[0, c], sibling)

    def pair_sum(c, hh):
        return acc[c, core, hh] + rb[c, hh].astype(F32)

    def core_sum(c):
        arrived(rb.at[c], t_recv.at[0, c])
        yb[c] = pair_sum(c, 1 - yh).astype(BF16)
        send(yb.at[c], yr.at[c], YB, t_recv.at[1, c], partner)

    def activate(c):
        arrived(yr.at[c], t_recv.at[1, c])
        total = pair_sum(c, yh) + yr[c].astype(F32)
        gate, up = total[0:FH], total[FH : 2 * FH]
        route = rt[c, yh]
        diff = route[3:4] - route[2:3]
        w = 1.0 / (1.0 + jnp.exp(jnp.where(core == 0, diff, -diff)))
        hb[c, core, yh] = (gate / (1.0 + jnp.exp(-gate)) * up * w).astype(BF16)
        mine = hb.at[c, core, yh]
        send(mine, mine, HB, t_recv.at[2, c], partner)
        send(mine, mine, HB, t_recv.at[3, c], sibling)

    def pass_on(c):
        theirs = hb.at[c, core, 1 - yh]
        arrived(theirs, t_recv.at[2, c])
        send(theirs, theirs, HB, t_recv.at[3, c], sibling)

    def down(c):
        arrived(hb.at[c, 1 - core], t_recv.at[3, c])
        pad = jnp.zeros((256 - FH, 128), F32)
        for hh in (0, 1):
            here = slice(hh * 128, (hh + 1) * 128)
            route = rt[c, hh].T
            units = [jnp.concatenate([hb[c, k, hh].astype(F32), pad], axis=0).T for k in (0, 1)]
            for e in range(E):
                both = jnp.where(route[:, 0:1] == float(e), units[0], 0.0)
                both = jnp.where(route[:, 1:2] == float(e), units[1], both)
                am[here, e * 256 : (e + 1) * 256] = both.astype(BF16)
        for j in range(4):
            w = dw[:, :, j * 256 : (j + 1) * 256].reshape(E * 256, 256)
            o = jnp.dot(am[...], w, preferred_element_type=F32)
            half, at = j // 2, (j % 2) * 256
            part[half, 2 * c : 2 * c + 2, :, :, :, at : at + 256] = o.astype(BF16).reshape(2, 2, 4, 16, 256)
        two = pl.ds(2 * c, 2)
        for half, first in ((0, xa), (1, xb)):
            for j, at in ((1, xd), (0, first)):
                send(part.at[half, two, :, at], r1.at[half, two, :, j], X1, x_recv.at[j, c], dev(fid(z, y, first), t))

    def x_first(c):
        two = pl.ds(2 * c, 2)
        arrived(r1.at[:, two, :, 1], x_recv.at[1, c])
        for half, second in ((0, xb), (1, xa)):
            s2[half, two] = (part[half, two, :, second].astype(F32) + r1[half, two, :, 1].astype(F32)).astype(BF16)
            send(s2.at[half, two], r2.at[half, two], X2, x_recv.at[2, c], dev(fid(z, y, second), t))

    def x_second(c):
        two = pl.ds(2 * c, 2)
        arrived(r1.at[:, two, :, 0], x_recv.at[0, c])
        arrived(r2.at[:, two], x_recv.at[2, c])
        for half in (0, 1):
            total = part[half, two, :, x].astype(F32) + r1[half, two, :, 0].astype(F32) + r2[half, two].astype(F32)
            zs[two, :, half] = total.astype(BF16)
        for at in (2 * c, 2 * c + 1):
            for dy in (0, 1):
                if OFFSETS[at] or dy:
                    yy = (y + dy) % 2
                    to = dev(fid(zoff(OFFSETS[at]), yy, x), t)
                    send(zs.at[at, yy], rz.at[2 * at + dy], Z, z_recv, to)

    def finish():
        arrived(rz.at[pl.ds(0, 15)], z_recv)
        total = zs[own, y].astype(F32)
        for i in range(16):
            if i != 2 * own:
                total = total + rz[i].astype(F32)
        for half in (0, 1):
            out_ref[:, half * HW : (half + 1) * HW] = total[half].astype(BF16)

    def leave():
        all_sent(xbuf.reshape(64, 16, DK).at[pl.ds(0, 63)], G)
        all_sent(rbuf.reshape(64, 1, 128).at[pl.ds(0, 63)], H)
        all_sent(pb, PB)
        all_sent(yb, YB)
        all_sent(hb.at[pl.ds(0, 3)], HB)
        all_sent(r1, X1)
        all_sent(s2, X2)
        all_sent(rz.at[pl.ds(0, 15)], Z)

    schedule = (
        (enter,),
        (spread,),
        (turn_scales,),
        (scale_gate_up, 0, 6),
        (along_x, 0), (along_x, 1),
        (scale_gate_up, 6, 8),
        (along_x, 7),
        (scale_down, 0, 3),
        (along_x, 2), (along_x, 3),
        (along_x_again, 0), (along_x_again, 1),
        (along_x, 4),
        (scale_down, 3, 6),
        (along_x, 5), (along_x, 6),
        (along_x_again, 2), (along_x_again, 3),
        (gate_up, 0),
        (along_x_again, 4), (along_x_again, 7),
        (core_sum, 0),
        (along_x_again, 5), (along_x_again, 6),
        (gate_up, 1),
        (core_sum, 1),
        (scale_down, 6, 8),
        (gate_up, 2),
        (activate, 0), (core_sum, 2),
        (gate_up, 3),
        (pass_on, 0), (activate, 1),
        (core_sum, 3),
        (down, 0),
        (activate, 2), (pass_on, 1),
        (down, 1),
        (activate, 3), (pass_on, 2),
        (x_first, 0),
        (down, 2),
        (x_first, 1),
        (pass_on, 3),
        (x_second, 0),
        (down, 3),
        (x_first, 2),
        (x_second, 1),
        (x_first, 3),
        (x_second, 2),
        (x_second, 3),
        (finish,),
        (leave,),
    )
    for step, *args in schedule:
        with jax.named_scope("_".join([step.__name__, *map(str, args)])):
            step(*args)


def body(tokens, logits, ids, gate_codes, gate_scales, up_codes, up_scales, down_codes, down_scales):
    vmem = pl.BlockSpec(memory_space=pltpu.VMEM)
    hbm = pl.BlockSpec(memory_space=pl.ANY)
    sems = pltpu.SemaphoreType.DMA
    return pl.pallas_call(
        kernel,
        out_shape=jax.ShapeDtypeStruct((16, DK), BF16),
        in_specs=[vmem] * 3 + [hbm] * 6,
        out_specs=vmem,
        scratch_shapes=[
            pltpu.VMEM((E, 2 * FH, DK), BF16),
            pltpu.VMEM((E, 256, DK), BF16),
            pltpu.VMEM((3, E, 8, FH), F32),
            pltpu.VMEM((FH, 128), F32),
            pltpu.VMEM((FH, 128), F32),
            pltpu.VMEM((8, 128), F32),
            pltpu.VMEM((8, 2, 4, 16, DK), BF16),
            pltpu.VMEM((8, 2, 4, 1, 128), F32),
            pltpu.VMEM((DK, 256), BF16),
            pltpu.VMEM((4, 2, 2, 2 * FH, 128), F32),
            pltpu.VMEM((4, 2, 8, 128), F32),
            pltpu.VMEM((4, 2, 2 * FH, 128), BF16),
            pltpu.VMEM((4, 2, 2 * FH, 128), BF16),
            pltpu.VMEM((4, 2 * FH, 128), BF16),
            pltpu.VMEM((4, 2 * FH, 128), BF16),
            pltpu.VMEM((4, 2, 2, FH, 128), BF16),
            pltpu.VMEM((256, E * 256), BF16),
            pltpu.VMEM((2, 8, 2, 4, 16, HW), BF16),
            pltpu.VMEM((2, 8, 2, 2, 16, HW), BF16),
            pltpu.VMEM((2, 8, 2, 16, HW), BF16),
            pltpu.VMEM((2, 8, 2, 16, HW), BF16),
            pltpu.VMEM((8, 2, 2, 16, HW), BF16),
            pltpu.VMEM((16, 2, 16, HW), BF16),
            sems((6,)),
            sems((8,)),
            sems((3, 8)),
            sems((3, 8)),
            sems((4, 4)),
            sems((3, 4)),
            sems,
        ],
        compiler_params=pltpu.CompilerParams(
            collective_id=0, has_side_effects=True, vmem_limit_bytes=60 * 1024 * 1024
        ),
        name="expert_step",
    )(
        tokens, logits.T, ids.T, gate_codes, jnp.swapaxes(gate_scales, 1, 2),
        up_codes, jnp.swapaxes(up_scales, 1, 2), down_codes, jnp.swapaxes(down_scales, 1, 2),
    )


def solution(mesh):
    wide = P(None, "fsdp", "tp")
    in_specs = (P("fsdp", "tp"), P("fsdp", None), P("fsdp", None)) + (wide,) * 6
    return jax.shard_map(body, mesh=mesh, in_specs=in_specs, out_specs=P("fsdp", "tp"), check_vma=False)
```

time: 100 us -> 79.9 us (0.80)
  the two profiles are of different devices: /device:TPU:104 before, /device:TPU:1 now
where the time goes in v2:
time: 79.9 us; the launch traced here: 79.6 us
  Pallas kernels  78.3 us (98%)
  local copies, waits for them, and re-layouts  1.38 us (2%)
    pallas_call x1, Pallas kernels, body(): pl.pallas_call(kernel, out_shape=jax.ShapeDtypeStruct((16, DK), BF16), in...  78.3 us

profile of v2, /device:TPU:1, one launch (start us, length us, event | category | flops | bytes accessed | tf_op | source)
XLA Modules:
  0.0 79.6 jit_solution(12991237740423115580)
XLA Ops:
  0.0 78.3 %expert_step.1 = bf16[16,1024]{1,0:T(8,128)(2,1)} custom-call(bf16[16,1024]{1,0:T(8,128)(2,1)} %tok_ref.1, bf16[2,16]{1,0:T(2,128)(2,1)} %bitcast.9, s32[2,16]{1,0:T(2,128)} %bitcast.8, bf16[8,224,1024]{2,1,0:T(8,128)(2,1)} %gc_ref.1, f32[8,8,224]{2,1,0:T(8,128)} %bitcast.5, bf16[8,224,1024]{2,1,0:T(8,128)(2,1)} %uc_ref.1, f32[8,8,224]{2,1,0:T(8,128)} %bitcast.6, ...), custom_call_target="tpu_custom_call" | custom-call | tf_op jit(solution)/shard_map/expert_step/pallas_call | solution.py:328
  78.3 1.4 %copy.11 = bf16[16,1024]{1,0:T(8,128)(2,1)} copy(bf16[16,1024]{1,0:T(8,128)(2,1)} %expert_step.1) | data formatting | bytes 65536

commit v3 on v2

--- a/solution.py
+++ b/solution.py
@@ -10,7 +10,7 @@
 E, FH, DK = 8, 224, 1024
 GROUP = 4
 HW = DK // 2
-OFFSETS = (1, -1, 3, -3, 4, 2, -2, 0)
+OFFSETS = (2, -2, 3, -3, 4, -1, 1, 0)
 
 
 def pos_of(r):
@@ -32,6 +32,7 @@
     xd = 3 - xa
     left, right, far = (x + 3) % 4, (x + 1) % 4, (x + 2) % 4
     own = pos_of(0)
+    nought = f // 64
 
     def fid(zz, yy, xx):
         return (zz * 2 + yy) * 4 + xx
@@ -98,6 +99,8 @@
     low, high = slice(0, HW), slice(HW, DK)
 
     def spread():
+        for to in (right, left):
+            both((own, y, x), (own, y, x), 1, own, dev(fid(z, y, to), t))
         for at, r in enumerate(OFFSETS):
             for dy in (0, 1):
                 if r or dy:
@@ -108,7 +111,7 @@
         arrived(xbuf.at[at, rows, x], g_recv.at[0, at])
         arrived(rbuf.at[at, rows, x], h_recv.at[0, at])
         for to in (right, left):
-            both((at, every, x), (at, every, x), 1, at, dev(fid(z, y, to), t))
+            both((at, rows, x), (at, rows, x), 1, at, dev(fid(z, y, to), t))
 
     def along_x_again(at):
         arrived(xbuf.at[at, 0], g_recv.at[1, at])
@@ -164,14 +167,14 @@
                 w = dw[e, 0:FH, cols].astype(F32) * scales[:, b : b + 1]
                 dw[e, 0:FH, cols] = w.astype(BF16)
 
-    def gate_up(c):
-        for hh in (0, 1):
-            plane_complete(2 * c + hh)
-            unpack_routes(2 * c + hh)
-        xt[...] = xbuf[2 * c : 2 * c + 2].reshape(256, DK).T
-        picks = [[rt[c, hh, k : k + 1, :] for hh in (0, 1)] for k in (0, 1)]
-
-        @pl.loop(0, E // GROUP)
+    def gate_up(c, g):
+        if g == 0:
+            for hh in (0, 1):
+                plane_complete(2 * c + hh)
+                unpack_routes(2 * c + hh)
+            xt[...] = xbuf[2 * c : 2 * c + 2].reshape(256, DK).T
+
+        @pl.loop(g + nought, g + 1 + nought)
         def _(g):
             w = wgu[pl.ds(g * GROUP, GROUP)].reshape(GROUP * 2 * FH, DK)
             o = jnp.dot(w, xt[...], preferred_element_type=F32)
@@ -180,38 +183,34 @@
                 for k in (0, 1):
                     for hh in (0, 1):
                         mine = o[i * 2 * FH : (i + 1) * 2 * FH, hh * 128 : (hh + 1) * 128]
-                        acc[c, k, hh] = jnp.where(picks[k][hh] == e, mine, acc[c, k, hh])
-
-        pb[c] = acc[c, 1 - core].astype(BF16)
-        send(pb.at[c], rb.at[c], PB, t_recv.at[0, c], sibling)
+                        acc[c, k, hh] = jnp.where(rt[c, hh, k : k + 1, :] == e, mine, acc[c, k, hh])
+
+        if g == E // GROUP - 1:
+            pb[c] = acc[c, 1 - core].astype(BF16)
+            send(pb.at[c], rb.at[c], PB, t_recv.at[0, c], sibling)
 
     def pair_sum(c, hh):
         return acc[c, core, hh] + rb[c, hh].astype(F32)
 
     def core_sum(c):
         arrived(rb.at[c], t_recv.at[0, c])
-        yb[c] = pair_sum(c, 1 - yh).astype(BF16)
+        for hh in (0, 1):
+            yb[c, hh] = pair_sum(c, hh).astype(BF16)
         send(yb.at[c], yr.at[c], YB, t_recv.at[1, c], partner)
 
     def activate(c):
         arrived(yr.at[c], t_recv.at[1, c])
-        total = pair_sum(c, yh) + yr[c].astype(F32)
-        gate, up = total[0:FH], total[FH : 2 * FH]
-        route = rt[c, yh]
-        diff = route[3:4] - route[2:3]
-        w = 1.0 / (1.0 + jnp.exp(jnp.where(core == 0, diff, -diff)))
-        hb[c, core, yh] = (gate / (1.0 + jnp.exp(-gate)) * up * w).astype(BF16)
-        mine = hb.at[c, core, yh]
-        send(mine, mine, HB, t_recv.at[2, c], partner)
-        send(mine, mine, HB, t_recv.at[3, c], sibling)
-
-    def pass_on(c):
-        theirs = hb.at[c, core, 1 - yh]
-        arrived(theirs, t_recv.at[2, c])
-        send(theirs, theirs, HB, t_recv.at[3, c], sibling)
+        for hh in (0, 1):
+            total = pair_sum(c, hh) + yr[c, hh].astype(F32)
+            gate, up = total[0:FH], total[FH : 2 * FH]
+            route = rt[c, hh]
+            diff = route[3:4] - route[2:3]
+            w = 1.0 / (1.0 + jnp.exp(jnp.where(core == 0, diff, -diff)))
+            hb[c, core, hh] = (gate / (1.0 + jnp.exp(-gate)) * up * w).astype(BF16)
+        send(hb.at[c, core], hb.at[c, core], HB, t_recv.at[2, c], sibling)
 
     def down(c):
-        arrived(hb.at[c, 1 - core], t_recv.at[3, c])
+        arrived(hb.at[c, 1 - core], t_recv.at[2, c])
         pad = jnp.zeros((256 - FH, 128), F32)
         for hh in (0, 1):
             here = slice(hh * 128, (hh + 1) * 128)
@@ -221,27 +220,32 @@
                 both = jnp.where(route[:, 0:1] == float(e), units[0], 0.0)
                 both = jnp.where(route[:, 1:2] == float(e), units[1], both)
                 am[here, e * 256 : (e + 1) * 256] = both.astype(BF16)
+        two = pl.ds(2 * c, 2)
         for j in range(4):
             w = dw[:, :, j * 256 : (j + 1) * 256].reshape(E * 256, 256)
             o = jnp.dot(am[...], w, preferred_element_type=F32)
             half, at = j // 2, (j % 2) * 256
             part[half, 2 * c : 2 * c + 2, :, :, :, at : at + 256] = o.astype(BF16).reshape(2, 2, 4, 16, 256)
+            if j % 2:
+                to = dev(fid(z, y, (xa, xb)[half]), t)
+                send(part.at[half, two, :, xd], r1.at[half, two, :, 1], X1, x_recv.at[half, c], to)
+
+    def x_rest(c):
         two = pl.ds(2 * c, 2)
-        for half, first in ((0, xa), (1, xb)):
-            for j, at in ((1, xd), (0, first)):
-                send(part.at[half, two, :, at], r1.at[half, two, :, j], X1, x_recv.at[j, c], dev(fid(z, y, first), t))
+        for half, to in ((0, xa), (1, xb)):
+            send(part.at[half, two, :, to], r1.at[half, two, :, 0], X1, x_recv.at[2, c], dev(fid(z, y, to), t))
 
     def x_first(c):
         two = pl.ds(2 * c, 2)
-        arrived(r1.at[:, two, :, 1], x_recv.at[1, c])
         for half, second in ((0, xb), (1, xa)):
+            arrived(r1.at[half, two, :, 1], x_recv.at[half, c])
             s2[half, two] = (part[half, two, :, second].astype(F32) + r1[half, two, :, 1].astype(F32)).astype(BF16)
-            send(s2.at[half, two], r2.at[half, two], X2, x_recv.at[2, c], dev(fid(z, y, second), t))
+            send(s2.at[half, two], r2.at[half, two], X2, x_recv.at[3, c], dev(fid(z, y, second), t))
 
     def x_second(c):
         two = pl.ds(2 * c, 2)
-        arrived(r1.at[:, two, :, 0], x_recv.at[0, c])
-        arrived(r2.at[:, two], x_recv.at[2, c])
+        arrived(r1.at[:, two, :, 0], x_recv.at[2, c])
+        arrived(r2.at[:, two], x_recv.at[3, c])
         for half in (0, 1):
             total = part[half, two, :, x].astype(F32) + r1[half, two, :, 0].astype(F32) + r2[half, two].astype(F32)
             zs[two, :, half] = total.astype(BF16)
@@ -266,7 +270,7 @@
         all_sent(rbuf.reshape(64, 1, 128).at[pl.ds(0, 63)], H)
         all_sent(pb, PB)
         all_sent(yb, YB)
-        all_sent(hb.at[pl.ds(0, 3)], HB)
+        all_sent(hb.at[pl.ds(0, 2)], HB)
         all_sent(r1, X1)
         all_sent(s2, X2)
         all_sent(rz.at[pl.ds(0, 15)], Z)
@@ -279,39 +283,47 @@
         (along_x, 0), (along_x, 1),
         (scale_gate_up, 6, 8),
         (along_x, 7),
-        (scale_down, 0, 3),
-        (along_x, 2), (along_x, 3),
+        (scale_down, 0, 2),
+        (along_x, 2),
+        (scale_down, 2, 3),
+        (along_x, 3),
         (along_x_again, 0), (along_x_again, 1),
         (along_x, 4),
         (scale_down, 3, 6),
-        (along_x, 5), (along_x, 6),
+        (along_x, 5),
         (along_x_again, 2), (along_x_again, 3),
-        (gate_up, 0),
-        (along_x_again, 4), (along_x_again, 7),
+        (along_x, 6),
+        (gate_up, 0, 0),
+        (along_x_again, 7), (along_x_again, 4),
+        (gate_up, 0, 1),
+        (along_x_again, 5),
+        (scale_down, 6, 8),
         (core_sum, 0),
-        (along_x_again, 5), (along_x_again, 6),
-        (gate_up, 1),
+        (gate_up, 1, 0),
+        (along_x_again, 6),
+        (gate_up, 1, 1),
+        (gate_up, 2, 0),
         (core_sum, 1),
-        (scale_down, 6, 8),
-        (gate_up, 2),
-        (activate, 0), (core_sum, 2),
-        (gate_up, 3),
-        (pass_on, 0), (activate, 1),
+        (gate_up, 2, 1),
+        (gate_up, 3, 0),
+        (core_sum, 2),
+        (gate_up, 3, 1),
+        (activate, 0),
         (core_sum, 3),
-        (down, 0),
-        (activate, 2), (pass_on, 1),
-        (down, 1),
-        (activate, 3), (pass_on, 2),
+        (down, 0), (x_rest, 0),
+        (activate, 1),
+        (down, 1), (x_rest, 1),
         (x_first, 0),
-        (down, 2),
+        (activate, 2),
+        (down, 2), (x_rest, 2),
         (x_first, 1),
-        (pass_on, 3),
         (x_second, 0),
-        (down, 3),
+        (activate, 3),
         (x_first, 2),
+        (down, 3), (x_rest, 3),
         (x_second, 1),
+        (x_second, 2),
         (x_first, 3),
-        (x_second, 2),
         (x_second, 3),
         (finish,),
         (leave,),
@@ -344,8 +356,8 @@
             pltpu.VMEM((4, 2, 8, 128), F32),
             pltpu.VMEM((4, 2, 2 * FH, 128), BF16),
             pltpu.VMEM((4, 2, 2 * FH, 128), BF16),
-            pltpu.VMEM((4, 2 * FH, 128), BF16),
-            pltpu.VMEM((4, 2 * FH, 128), BF16),
+            pltpu.VMEM((4, 2, 2 * FH, 128), BF16),
+            pltpu.VMEM((4, 2, 2 * FH, 128), BF16),
             pltpu.VMEM((4, 2, 2, FH, 128), BF16),
             pltpu.VMEM((256, E * 256), BF16),
             pltpu.VMEM((2, 8, 2, 4, 16, HW), BF16),
@@ -358,8 +370,8 @@
             sems((8,)),
             sems((3, 8)),
             sems((3, 8)),
+            sems((3, 4)),
             sems((4, 4)),
-            sems((3, 4)),
             sems,
         ],
         compiler_params=pltpu.CompilerParams(

time: 79.9 us -> 76.4 us (0.956)
  Pallas kernels: 78.3 us -> 74.8 us
    pallas_call x1, Pallas kernels: 78.3 us -> 74.8 us  [body(): pl.pallas_call(kernel, out_shape=jax.ShapeDtypeStruct((16, DK), BF16), in...]
where the time goes in v3:
time: 76.4 us; the launch traced here: 76.2 us
  Pallas kernels  74.8 us (98%)
  local copies, waits for them, and re-layouts  1.38 us (2%)
    pallas_call x1, Pallas kernels, body(): pl.pallas_call(kernel, out_shape=jax.ShapeDtypeStruct((16, DK), BF16), in...  74.8 us

profile of v3, /device:TPU:1, one launch (start us, length us, event | category | flops | bytes accessed | tf_op | source)
XLA Modules:
  0.0 76.2 jit_solution(15821925440752488170)
XLA Ops:
  0.0 74.8 %expert_step.1 = bf16[16,1024]{1,0:T(8,128)(2,1)} custom-call(bf16[16,1024]{1,0:T(8,128)(2,1)} %tok_ref.1, bf16[2,16]{1,0:T(2,128)(2,1)} %bitcast.9, s32[2,16]{1,0:T(2,128)} %bitcast.8, bf16[8,224,1024]{2,1,0:T(8,128)(2,1)} %gc_ref.1, f32[8,8,224]{2,1,0:T(8,128)} %bitcast.5, bf16[8,224,1024]{2,1,0:T(8,128)(2,1)} %uc_ref.1, f32[8,8,224]{2,1,0:T(8,128)} %bitcast.6, ...), custom_call_target="tpu_custom_call" | custom-call | tf_op jit(solution)/shard_map/expert_step/pallas_call | solution.py:340
  74.8 1.4 %copy.11 = bf16[16,1024]{1,0:T(8,128)(2,1)} copy(bf16[16,1024]{1,0:T(8,128)(2,1)} %expert_step.1) | data formatting | bytes 65536

commit v4 on v3

--- a/solution.py
+++ b/solution.py
@@ -11,6 +11,7 @@
 GROUP = 4
 HW = DK // 2
 OFFSETS = (2, -2, 3, -3, 4, -1, 1, 0)
+DIRECT = (0, 1)
 
 
 def pos_of(r):
@@ -64,7 +65,7 @@
 
     barrier = pltpu.get_barrier_semaphore()
     friends = [dev(fid(zoff(r), (y + dy) % 2, x), t) for r in OFFSETS for dy in (0, 1) if r or dy]
-    friends += [dev(fid(z, y, left), t), dev(fid(z, y, right), t), sibling, partner]
+    friends += [dev(fid(z, y, xx), t) for xx in (left, right, far)] + [sibling, partner]
     for to in friends:
         pl.semaphore_signal(barrier, inc=1, device_id=to, device_id_type=MESH)
 
@@ -112,10 +113,14 @@
         arrived(rbuf.at[at, rows, x], h_recv.at[0, at])
         for to in (right, left):
             both((at, rows, x), (at, rows, x), 1, at, dev(fid(z, y, to), t))
+        if at in DIRECT:
+            both((at, every, x), (at, every, x), 2, at, dev(fid(z, y, far), t))
 
     def along_x_again(at):
         arrived(xbuf.at[at, 0], g_recv.at[1, at])
         arrived(rbuf.at[at, 0], h_recv.at[1, at])
+        if at in DIRECT:
+            return
         here = (at, every, left, every, low)
         both(here, here, 2, at, dev(fid(z, y, right), t))
         here = (at, every, right, every, high)
@@ -287,15 +292,15 @@
         (along_x, 2),
         (scale_down, 2, 3),
         (along_x, 3),
-        (along_x_again, 0), (along_x_again, 1),
         (along_x, 4),
         (scale_down, 3, 6),
         (along_x, 5),
-        (along_x_again, 2), (along_x_again, 3),
         (along_x, 6),
+        (along_x_again, 0), (along_x_again, 1),
         (gate_up, 0, 0),
-        (along_x_again, 7), (along_x_again, 4),
+        (along_x_again, 2), (along_x_again, 3), (along_x_again, 7),
         (gate_up, 0, 1),
+        (along_x_again, 4),
         (along_x_again, 5),
         (scale_down, 6, 8),
         (core_sum, 0),

time: 76.4 us -> 75.6 us (0.990)
  Pallas kernels: 74.8 us -> 74 us
    pallas_call x1, Pallas kernels: 74.8 us -> 74 us  [body(): pl.pallas_call(kernel, out_shape=jax.ShapeDtypeStruct((16, DK), BF16), in...]
where the time goes in v4:
time: 75.6 us; the launch traced here: 75.4 us
  Pallas kernels  74 us (98%)
  local copies, waits for them, and re-layouts  1.38 us (2%)
    pallas_call x1, Pallas kernels, body(): pl.pallas_call(kernel, out_shape=jax.ShapeDtypeStruct((16, DK), BF16), in...  74 us

profile of v4, /device:TPU:1, one launch (start us, length us, event | category | flops | bytes accessed | tf_op | source)
XLA Modules:
  0.0 75.4 jit_solution(2607140806645313987)
XLA Ops:
  0.0 74.0 %expert_step.1 = bf16[16,1024]{1,0:T(8,128)(2,1)} custom-call(bf16[16,1024]{1,0:T(8,128)(2,1)} %tok_ref.1, bf16[2,16]{1,0:T(2,128)(2,1)} %bitcast.9, s32[2,16]{1,0:T(2,128)} %bitcast.8, bf16[8,224,1024]{2,1,0:T(8,128)(2,1)} %gc_ref.1, f32[8,8,224]{2,1,0:T(8,128)} %bitcast.5, bf16[8,224,1024]{2,1,0:T(8,128)(2,1)} %uc_ref.1, f32[8,8,224]{2,1,0:T(8,128)} %bitcast.6, ...), custom_call_target="tpu_custom_call" | custom-call | tf_op jit(solution)/shard_map/expert_step/pallas_call | solution.py:345
  74.0 1.4 %copy.11 = bf16[16,1024]{1,0:T(8,128)(2,1)} copy(bf16[16,1024]{1,0:T(8,128)(2,1)} %expert_step.1) | data formatting | bytes 65536
